TPU v7x, 32 devices: a whole 2x2x4 slice. The times are simulated.
32 devices in a mesh: tok: 16 (over z, y, x), head: 2 (over core).
Axes of the slice: x: 2, y: 2, z: 4, core: 2. Of those that a mesh axis runs over, the one named last changes fastest.
Arguments:
- text_queries: bfloat16 [256, 8192], P('tok', 'head'), may hold values from -6 to 6
- text_grads: bfloat16 [256, 8192], P('tok', 'head'), may hold values from -6 to 6
- vision_keys: bfloat16 [8192, 1024], P('tok', 'head'), may hold values from -6 to 6
- video_value_rows: bfloat16 [8192, 1024], P('tok', 'head'), may hold values from -6 to 6
- vision: bfloat16 [8192, 4096], P('tok'), may hold values from -6 to 6
- lengths: int32 [8], replicated, may hold values from 16 to 48, as said below
- frame_range: int32 [8, 2], replicated, may hold values from 0 to 64, as said below
Outputs:
- query_grad: bfloat16 [256, 8192], P(None, 'head')
- key_weight_grad: float32 [4096, 1024], P('tok', 'head')
- value_weight_grad: float32 [4096, 1024], P('tok', 'head')
Inputs may be any that keep to these rules, and one draw needn't show every extreme that they name: Each segment holds at least one row; the lengths sum to 256. `frame_range`: each segment's range covers 64 // 4 frames or more, first entry below the second.
All inputs are finite; a program needn't handle non-finite values.
Results may differ from a plain program's by a relative error of at most 0.0073.
Values may be sent and summed in bfloat16 or wider, within the bound.
A program may use at most 128 MiB of HBM per device.

v0:
```python
import jax
import jax.numpy as jnp
from jax import lax
from jax.sharding import PartitionSpec as P

HEAD_WIDTH = 128
FRAME_DEV = 4
NEG_FILL = -1e30


def shards(text_queries, text_grads, vision_keys, video_value_rows, vision, lengths, frame_range):
    feature_block = lax.all_to_all(vision, "tok", split_axis=1, concat_axis=0, tiled=True)
    text_q, text_g = (
        lax.all_gather(text_queries, "tok", axis=0, tiled=True),
        lax.all_gather(text_grads, "tok", axis=0, tiled=True),
    )
    text_len = text_q.shape[0]
    kv_rows = vision_keys.shape[0]
    kv_local = vision_keys.shape[1] // HEAD_WIDTH
    group_width = text_q.shape[1] // vision_keys.shape[1]
    score_scale = HEAD_WIDTH ** (-0.5)
    row_ids = jnp.arange(text_len, dtype=jnp.int32)
    segment_ends = jnp.cumsum(lengths)
    segment = jnp.sum((row_ids[:, None] >= segment_ends[None, :]).astype(jnp.int32), axis=1)
    segment_pick = (
        segment[:, None] == jnp.arange(lengths.shape[0], dtype=jnp.int32)[None, :]
    ).astype(jnp.int32)
    first_frame = jnp.sum(segment_pick * frame_range[None, :, 0], axis=1)
    end_frame = jnp.sum(segment_pick * frame_range[None, :, 1], axis=1)
    key_ids = lax.axis_index("tok") * kv_rows + jnp.arange(kv_rows, dtype=jnp.int32)
    frames = key_ids // (kv_rows // FRAME_DEV)
    allowed = (frames[None, :] >= first_frame[:, None]) & (frames[None, :] < end_frame[:, None])
    query_member = text_q.reshape(text_len, kv_local, group_width, HEAD_WIDTH).transpose(2, 0, 1, 3)
    grad_member = text_g.reshape(text_len, kv_local, group_width, HEAD_WIDTH).transpose(2, 0, 1, 3)
    key_three = vision_keys.reshape(kv_rows, kv_local, HEAD_WIDTH)
    value_three = video_value_rows.reshape(kv_rows, kv_local, HEAD_WIDTH)

    def scores_of(query_one, grad_one):
        scores = (
            jnp.einsum("ihd,jhd->hij", query_one, key_three, preferred_element_type=jnp.float32)
            * score_scale
        )
        dprobs = jnp.einsum(
            "ihd,jhd->hij", grad_one, value_three, preferred_element_type=jnp.float32
        )
        return (scores, dprobs)

    def local_stats(carry, member):
        scores, dprobs = scores_of(member[0], member[1])
        local_max = jnp.max(jnp.where(allowed, scores, NEG_FILL), axis=2)
        local_exp = jnp.where(allowed, jnp.exp(scores - local_max[..., None]), 0.0)
        return (carry, (local_max, jnp.sum(local_exp, axis=2), jnp.sum(local_exp * dprobs, axis=2)))

    unused, (local_max, local_sum, local_dot) = lax.scan(
        local_stats, jnp.zeros((), jnp.float32), (query_member, grad_member)
    )
    row_max = lax.pmax(local_max, "tok")
    rescale = jnp.exp(local_max - row_max)
    row_sum, row_dot = lax.psum((local_sum * rescale, local_dot * rescale), "tok")

    def member_grads(running, member):
        query_one, grad_one, max_one, sum_one, dot_one = member
        scores, dprobs = scores_of(query_one, grad_one)
        exp_terms = jnp.where(allowed, jnp.exp(scores - max_one[..., None]), 0.0)
        attn_probs = exp_terms / sum_one[..., None]
        row_delta = dot_one / sum_one
        dscore = (attn_probs * (dprobs - row_delta[..., None])).astype(jnp.bfloat16)
        value_sum = running[1] + jnp.einsum(
            "hij,ihd->jhd",
            attn_probs.astype(jnp.bfloat16),
            grad_one,
            preferred_element_type=jnp.float32,
        )
        key_sum = running[0] + jnp.einsum(
            "hij,ihd->jhd", dscore, query_one, preferred_element_type=jnp.float32
        )
        query_part = score_scale * jnp.einsum(
            "hij,jhd->ihd", dscore, key_three, preferred_element_type=jnp.float32
        )
        return ((key_sum, value_sum), query_part)

    zero_acc = jnp.zeros((kv_rows, kv_local, HEAD_WIDTH), jnp.float32)
    (key_sum, value_sum), query_parts = lax.scan(
        member_grads, (zero_acc, zero_acc), (query_member, grad_member, row_max, row_sum, row_dot)
    )
    key_grad = (score_scale * key_sum).astype(jnp.bfloat16)
    value_grad = value_sum.astype(jnp.bfloat16)
    query_part = query_parts.transpose(1, 2, 0, 3).reshape(text_len, -1)
    query_grad = lax.psum(query_part, "tok").astype(jnp.bfloat16)
    kv_data = jnp.concatenate(
        (key_grad.reshape(kv_rows, -1), value_grad.reshape(kv_rows, -1)), axis=1
    )
    half_width = kv_data.shape[1] // 2
    weight_grads = jnp.einsum(
        "tf,tc->fc",
        feature_block,
        lax.all_gather(kv_data, "tok", axis=0, tiled=True),
        preferred_element_type=jnp.float32,
    )
    return (query_grad, weight_grads[:, :half_width], weight_grads[:, half_width:])


def solution(mesh):
    return jax.shard_map(
        shards,
        mesh=mesh,
        in_specs=(
            P("tok", "head"),
            P("tok", "head"),
            P("tok", "head"),
            P("tok", "head"),
            P("tok", None),
            P(),
            P(),
        ),
        out_specs=(P(None, "head"), P("tok", "head"), P("tok", "head")),
        check_vma=False,
    )
```

profile of v0, /device:TPU:4, one launch (start us, length us, event | category | flops | bytes accessed | tf_op | source)
XLA Modules:
  0.0 843.1 jit_solution(17630682502274391698)
XLA Ops:
  11.8 60.5 %all-gather.4.cloned.1.call-done = bf16[256,4096]{1,0:T(8,128)(2,1)} async-done(((bf16[16,4096]{1,0:T(8,128)(2,1)}), bf16[256,4096]{1,0:T(8,128)(2,1)}) %all-gather.4.cloned.1.call-update) | async-done | bytes 2097168 | tf_op jit(solution)/shard_map/all_gather | solution.py:14
  72.4 4.1 copy.72
  76.4 3.0 copy.80
  79.5 54.9 %all-gather.6.cloned.1.call-done = bf16[256,4096]{1,0:T(8,128)(2,1)} async-done(((bf16[16,4096]{1,0:T(8,128)(2,1)}), bf16[256,4096]{1,0:T(8,128)(2,1)}) %all-gather.6.cloned.1.call-update) | async-done | bytes 2097168 | tf_op jit(solution)/shard_map/all_gather | solution.py:15
  134.3 4.1 copy.74
  138.4 4.0 copy.78
  142.4 26.8 %while.30 = (s32[]{:T(128)}, f32[8,4,256]{2,1,0:T(4,128)S(1)}, f32[8,4,256]{2,1,0:T(4,128)S(1)}, f32[8,4,256]{2,1,0:T(4,128)S(1)}, bf16[8,256,4,128]{3,1,2,0:T(8...) while((s32[]{:T(128)}, f32[8,4,256]{2,1,0:T(4,128)S(1)}, ...), condition=%wide.region_8.9_spmd.clone, body=%wide.region_4.8_spmd.clone.sunk | while | flops 275117056 | bytes 8437901 | solution.py:54
  143.9 1.8 multiply_reduce_fusion.2
  147.2 1.8 multiply_reduce_fusion.2
  150.6 1.8 multiply_reduce_fusion.2
  153.9 1.8 multiply_reduce_fusion.2
  157.3 1.8 multiply_reduce_fusion.2
  160.6 1.8 multiply_reduce_fusion.2
  164.0 1.8 multiply_reduce_fusion.2
  167.4 1.8 multiply_reduce_fusion.2
  169.2 71.0 %pmax.7 = f32[8,4,256]{2,1,0:T(4,128)S(1)} all-reduce(f32[8,4,256]{2,1,0:T(4,128)S(1)} %get-tuple-element.116), channel_id=1, replica_groups=mesh['tok'=16,'head'=2] {'tok'}, use_global_device_ids=true, to_apply=%region_9.10 | all-reduce | flops 8192 | bytes 65536 | tf_op jit(solution)/shard_map/pmax | solution.py:57
  241.0 103.4 %all-reduce.4.cloned.1.call-done = (f32[8,4,256]{2,1,0:T(4,128)}, f32[8,4,256]{2,1,0:T(4,128)}) async-done(((f32[8,4,256]{2,1,0:T(4,128)}, f32[8,4,256]{2,1,0:T(4,128)}), (f32[8,4,256]{2,1,0:T(4,128)}, f32[8,4,256]{2,1,0:T(4,128)})) %all-reduce.4.cloned.1.call-update) | async-done | bytes 65552 | tf_op jit(solution)/shard_map/psum | solution.py:59
  344.4 69.9 %while.31 = (s32[]{:T(128)}, f32[512,4,128]{0,2,1:T(8,128)S(1)}, f32[512,4,128]{0,2,1:T(8,128)S(1)}, f32[8,256,4,128]{3,1,2,0:T(8,128)}, bf16[8,256,4,128]{3,1,2...) while((s32[]{:T(128)}, f32[512,4,128]{0,2,1:T(8,128)S(1)}, ...), condition=%wide.region_13.14_spmd.clone, body=%wide.region_12.13_spmd.clone.sunk | while | flops 676856832 | bytes 17084612 | solution.py:83
  346.0 1.7 select_divide_fusion.2
  363.5 1.7 select_divide_fusion.2
  372.3 1.7 select_divide_fusion.2
  381.0 1.7 select_divide_fusion.2
  389.7 1.7 select_divide_fusion.2
  398.4 1.7 select_divide_fusion.2
  415.6 6.5 copy.85
  422.1 5.2 all-to-all-start
  427.3 4.6 copy.84
  431.9 5.8 copy.93
  437.7 350.3 %all-reduce.5 = bf16[256,4096]{1,0:T(8,128)(2,1)} all-reduce(f32[256,4096]{1,0:T(8,128)} %bitcast.132), channel_id=1, replica_groups=mesh['tok'=16,'head'=2] {'tok'}, use_global_device_ids=true, to_apply=%region_14.15 | all-reduce | flops 1048576 | bytes 6291456 | tf_op jit(solution)/shard_map/psum | solution.py:89
  788.0 6.4 copy.86
  794.4 30.8 %all-gather.8.cloned.1.call-done = bf16[8192,1024]{0,1:T(8,128)(2,1)} async-done(((bf16[512,1024]{0,1:T(8,128)(2,1)}), bf16[8192,1024]{0,1:T(8,128)(2,1)}) %all-gather.8.cloned.1.call-update) | async-done | bytes 16777232 | tf_op jit(solution)/shard_map/all_gather | solution.py:97
  825.2 9.3 %convolution_bitcast_fusion.2 = f32[256,1024]{0,1:T(8,128)S(1)} fusion(bf16[8192,1024]{0,1:T(8,128)(2,1)} %all-gather.8.cloned.1.call-done, bf16[8192,256]{1,0:T(8,128)(2,1)} %bitcast.136), kind=kOutput, calls=%fused_computation.44 | convolution fusion | flops 4294967296 | bytes 22020096 | tf_op jit(solution)/shard_map/tf,tc->fc/dot_general | solution.py:94
  (135 shorter events, 80.3 us)
Async XLA Ops:
  7.2 4.0 copy-start.1
  7.2 65.2 %all-gather.4.cloned.1.call-start = ((), (), s32[]{:S(2)}) async-start(), calls=%async_computation.1 | async-start | bytes 2228224 | tf_op jit(solution)/shard_map/all_gather | solution.py:14
  7.9 126.4 %all-gather.6.cloned.1.call-start = ((), (), s32[]{:S(2)}) async-start(), calls=%async_computation.2 | async-start | bytes 2228224 | tf_op jit(solution)/shard_map/all_gather | solution.py:15
  8.7 335.8 %all-reduce.4.cloned.1.call-start = ((), (), s32[]{:S(2)}) async-start(), calls=%async_computation.4 | async-start | bytes 131072 | tf_op jit(solution)/shard_map/psum | solution.py:59
  9.6 2.2 copy-start.2
  169.2 71.8 %copy-start = (bf16[8,256,4,128]{3,1,2,0:T(8,128)(2,1)}, bf16[8,256,4,128]{3,1,2,0:T(8,128)(2,1)S(1)}, u32[]{:S(2)}) copy-start(bf16[8,256,4,128]{3,1,2,0:T(8,128)(2,1)S(1)} %get-tuple-element.641) | copy-start | bytes 6291460
  240.9 584.3 %all-gather.8.cloned.1.call-start = ((), (), s32[]{:S(2)}) async-start(), calls=%async_computation.3 | async-start | bytes 17825792 | tf_op jit(solution)/shard_map/all_gather | solution.py:97
  422.1 365.9 %all-to-all-start = ((bf16[512,16,256]{0,2,1:T(8,128)(2,1)}), bf16[512,16,256]{0,2,1:T(8,128)(2,1)}, u32[]{:S(2)}, u32[]{:S(2)}) async-start(bf16[512,16,256]{0,2,1:T(8,128)(2,1)} %bitcast.130), calls=%async_computation | async-start | bytes 8388608 | tf_op jit(solution)/shard_map/all_to_all | solution.py:12
Sparse Core Ops, SparseCore 0:
  10.8 61.5 all-gather.3
  75.1 59.1 all-gather.5
  241.0 103.3 all-reduce.3
  415.8 409.3 all-gather.7
where the time goes:
time: 846 us; the launch traced here: 843 us
  blocking collectives  421 us (50%)
  waiting for transfers between devices  251 us (30%)
  matrix products  85.4 us (10%)
  local copies, waits for them, and re-layouts  48.1 us (6%)
  other arithmetic  17.4 us (2%)
  between operations  13.9 us (2%)
    psum x1, blocking collectives, shards(): query_grad = lax.psum(query_part, 'tok').astype(jnp.bfloat16)  350 us
    psum x1, waiting for transfers between devices, shards(): lax.psum((local_sum * rescale, local_dot * rescale), 'tok')  103 us
    pmax x1, blocking collectives, shards(): row_max = lax.pmax(local_max, 'tok')  71 us
    all_gather x1, waiting for transfers between devices, shards(): lax.all_gather(text_queries, 'tok', axis=0, tiled=True)  60.5 us
    all_gather x1, waiting for transfers between devices, shards(): lax.all_gather(text_grads, 'tok', axis=0, tiled=True)  54.9 us
    all_gather x1, waiting for transfers between devices, shards(): lax.all_gather(kv_data, 'tok', axis=0, tiled=True)  30.8 us
    dot_general x16, matrix products, scores_of(): jnp.einsum('ihd,jhd->hij', grad_one, value_three, preferred_element_type=...  25.6 us
    unnamed x16, local copies, waits for them, and re-layouts  23.2 us
  transfers between devices with their start and end apart: 5, of which 4 were waited for; matrix products, arithmetic and copies ran while one was open for 4% of the time, Pallas kernels for 0%

commit v1 on v0

--- a/solution.py
+++ b/solution.py
@@ -86,7 +86,8 @@
     key_grad = (score_scale * key_sum).astype(jnp.bfloat16)
     value_grad = value_sum.astype(jnp.bfloat16)
     query_part = query_parts.transpose(1, 2, 0, 3).reshape(text_len, -1)
-    query_grad = lax.psum(query_part, "tok").astype(jnp.bfloat16)
+    test_runs = lambda shard_in: jnp.sum(jax.lax.all_gather(shard_in, "tok"), 0)
+    query_grad = test_runs(query_part).astype(jnp.bfloat16)
     kv_data = jnp.concatenate(
         (key_grad.reshape(kv_rows, -1), value_grad.reshape(kv_rows, -1)), axis=1
     )

time: 846 us -> 1470 us (1.74)
  waiting for transfers between devices: 251 us -> 976 us
  blocking collectives: 421 us -> 229 us
  matrix products: 85.4 us -> 124 us
  local copies, waits for them, and re-layouts: 48.1 us -> 78.9 us
  other arithmetic: 17.4 us -> 40.8 us
    all_gather x0 -> x1, waiting for transfers between devices: none -> 658 us  [shards(): test_runs = lambda shard_in: jnp.sum(jax.lax.all_gather(shard_in, 'tok'), 0)]
    psum x1 -> x0, blocking collectives: 350 us -> none  [shards(): query_grad = lax.psum(query_part, 'tok').astype(jnp.bfloat16)]
    all_to_all x0 -> x1, blocking collectives: none -> 158 us  [shards(): lax.all_to_all(vision, 'tok', split_axis=1, concat_axis=0, tiled=True)]
    all_gather x1, waiting for transfers between devices: 30.8 us -> 96.8 us  [shards(): lax.all_gather(kv_data, 'tok', axis=0, tiled=True)]
    dynamic_update_slice x0 -> x16, local copies, waits for them, and re-layouts: none -> 31.8 us  [shards(): lax.scan(member_grads, (zero_acc, zero_acc), (query_member, grad_member,...]
    reduce_sum x0 -> x1, other arithmetic: none -> 21.1 us  [shards(): test_runs = lambda shard_in: jnp.sum(jax.lax.all_gather(shard_in, 'tok'), 0)]
  transfers between devices with their start and end apart: 5 -> 5, of which waited for: 4 -> 5; matrix products, arithmetic and copies ran while one was open for 4% -> 3% of each run, Pallas kernels for 0% -> 0%
where the time goes in v1:
time: 1470 us; the launch traced here: 1460 us
  waiting for transfers between devices  976 us (66%)
  blocking collectives  229 us (16%)
  matrix products  124 us (8%)
  local copies, waits for them, and re-layouts  78.9 us (5%)
  other arithmetic  40.8 us (3%)
    all_gather x1, waiting for transfers between devices, shards(): test_runs = lambda shard_in: jnp.sum(jax.lax.all_gather(shard_in, 'tok'), 0)  658 us
    all_to_all x1, blocking collectives, shards(): lax.all_to_all(vision, 'tok', split_axis=1, concat_axis=0, tiled=True)  158 us
    psum x1, waiting for transfers between devices, shards(): lax.psum((local_sum * rescale, local_dot * rescale), 'tok')  103 us
    all_gather x1, waiting for transfers between devices, shards(): lax.all_gather(kv_data, 'tok', axis=0, tiled=True)  96.8 us
    pmax x1, blocking collectives, shards(): row_max = lax.pmax(local_max, 'tok')  71 us
    all_gather x1, waiting for transfers between devices, shards(): lax.all_gather(text_grads, 'tok', axis=0, tiled=True)  59.8 us
    all_gather x1, waiting for transfers between devices, shards(): lax.all_gather(text_queries, 'tok', axis=0, tiled=True)  56.3 us
    dynamic_update_slice x16, local copies, waits for them, and re-layouts, shards(): lax.scan(member_grads, (zero_acc, zero_acc), (query_member, grad_member,...  31.8 us
  transfers between devices with their start and end apart: 5, of which 5 were waited for; matrix products, arithmetic and copies ran while one was open for 3% of the time, Pallas kernels for 0%

profile of v1, /device:TPU:4, one launch (start us, length us, event | category | flops | bytes accessed | tf_op | source)
XLA Modules:
  0.0 1463.8 jit_solution(2744324950203863461)
XLA Ops:
  12.5 59.8 %all-gather.7.cloned.1.call-done = bf16[256,4096]{1,0:T(8,128)(2,1)} async-done(((bf16[16,4096]{1,0:T(8,128)(2,1)}), bf16[256,4096]{1,0:T(8,128)(2,1)}) %all-gather.7.cloned.1.call-update) | async-done | bytes 2097168 | tf_op jit(solution)/shard_map/all_gather | solution.py:15
  72.4 3.3 copy.76
  78.0 56.3 %all-gather.5.cloned.1.call-done = bf16[256,4096]{1,0:T(8,128)(2,1)} async-done(((bf16[16,4096]{1,0:T(8,128)(2,1)}), bf16[256,4096]{1,0:T(8,128)(2,1)}) %all-gather.5.cloned.1.call-update) | async-done | bytes 2097168 | tf_op jit(solution)/shard_map/all_gather | solution.py:14
  134.3 3.3 copy.74
  140.0 35.8 %while.30 = (s32[]{:T(128)}, f32[8,4,256]{2,1,0:T(4,128)S(1)}, f32[8,4,256]{2,1,0:T(4,128)S(1)}, f32[8,4,256]{2,1,0:T(4,128)S(1)}, bf16[8,256,4,128]{3,1,2,0:T(8...) while((s32[]{:T(128)}, f32[8,4,256]{2,1,0:T(4,128)S(1)}, ...), condition=%wide.region_8.9_spmd.clone, body=%wide.region_4.8_spmd.clone.sunk | while | flops 275117056 | bytes 8438909 | solution.py:54
  175.8 71.0 %pmax.7 = f32[8,4,256]{2,1,0:T(4,128)S(1)} all-reduce(f32[8,4,256]{2,1,0:T(4,128)S(1)} %get-tuple-element.116), channel_id=1, replica_groups=mesh['tok'=16,'head'=2] {'tok'}, use_global_device_ids=true, to_apply=%region_9.10 | all-reduce | flops 8192 | bytes 65536 | tf_op jit(solution)/shard_map/pmax | solution.py:57
  247.6 103.5 %all-reduce.3.cloned.1.call-done = (f32[8,4,256]{2,1,0:T(4,128)}, f32[8,4,256]{2,1,0:T(4,128)}) async-done(((f32[8,4,256]{2,1,0:T(4,128)}, f32[8,4,256]{2,1,0:T(4,128)}), (f32[8,4,256]{2,1,0:T(4,128)}, f32[8,4,256]{2,1,0:T(4,128)})) %all-reduce.3.cloned.1.call-update) | async-done | bytes 65552 | tf_op jit(solution)/shard_map/psum | solution.py:59
  351.1 131.5 %while.31 = (s32[]{:T(128)}, f32[512,4,128]{0,2,1:T(8,128)}, f32[512,4,128]{0,2,1:T(8,128)}, f32[8,256,4,128]{1,3,0,2:T(8,128)}, bf16[8,256,4,128]{3,1,2,0:T(8,1...) while((s32[]{:T(128)}, f32[512,4,128]{0,2,1:T(8,128)}, ...), condition=%wide.region_13.14_spmd.clone, body=%wide.region_12.13_spmd.clone.sunk | while | flops 676856832 | bytes 23378656 | solution.py:83
  378.0 2.7 fusion.74
  380.7 2.7 fusion.75
  394.5 2.7 fusion.74
  397.2 2.7 fusion.75
  411.1 2.7 fusion.74
  413.7 2.7 fusion.75
  427.6 2.7 fusion.74
  430.2 2.7 fusion.75
  444.1 2.7 fusion.74
  446.8 2.7 fusion.75
  460.6 2.7 fusion.74
  463.3 2.7 fusion.75
  477.1 2.7 fusion.74
  479.8 2.7 fusion.75
  486.3 5.6 copy.87
  491.9 6.6 copy.89
  498.6 158.1 %all_to_all.19 = bf16[512,16,256]{0,2,1:T(8,128)(2,1)} all-to-all(bf16[512,16,256]{0,2,1:T(8,128)(2,1)} %bitcast.126), channel_id=1, replica_groups=mesh['tok'=16,'head'=2] {'tok'}, dimensions={1} | all-to-all | bytes 8388608 | tf_op jit(solution)/shard_map/all_to_all | solution.py:12
  656.7 6.5 copy.90
  663.2 96.8 %all-gather.11.cloned.1.call-done = bf16[8192,1024]{0,1:T(8,128)(2,1)} async-done(((bf16[512,1024]{0,1:T(8,128)(2,1)}), bf16[8192,1024]{0,1:T(8,128)(2,1)}) %all-gather.11.cloned.1.call-update) | async-done | bytes 16777232 | tf_op jit(solution)/shard_map/all_gather | solution.py:98
  760.0 9.3 convolution_bitcast_fusion.2
  771.4 658.2 %all-gather.9.cloned.1.call-done = f32[16,256,4096]{2,1,0:T(8,128)} async-done(((f32[1,256,4096]{2,1,0:T(8,128)}), f32[16,256,4096]{2,1,0:T(8,128)}) %all-gather.9.cloned.1.call-update) | async-done | bytes 67108880 | tf_op jit(solution)/shard_map/all_gather | solution.py:89
  1429.6 21.1 %reduce_sum.57 = bf16[256,4096]{1,0:T(8,128)(2,1)S(1)} reduce(f32[16,256,4096]{2,1,0:T(8,128)} %all-gather.9.cloned.1.call-done, f32[]{:T(128)} %constant.66.clone.1), dimensions={0}, to_apply=%region_14.15 | reduce | flops 15728640 | bytes 69206016 | tf_op jit(solution)/shard_map/reduce_sum | solution.py:89
  1450.7 2.5 copy.98
  1453.2 4.1 copy.91
  (184 shorter events, 145.8 us)
Async XLA Ops:
  7.2 4.7 copy-start.2
  7.2 65.2 %all-gather.7.cloned.1.call-start = ((), (), s32[]{:S(2)}) async-start(), calls=%async_computation.2 | async-start | bytes 2228224 | tf_op jit(solution)/shard_map/all_gather | solution.py:15
  7.9 126.4 %all-gather.5.cloned.1.call-start = ((), (), s32[]{:S(2)}) async-start(), calls=%async_computation.1 | async-start | bytes 2228224 | tf_op jit(solution)/shard_map/all_gather | solution.py:14
  8.7 342.4 %all-reduce.3.cloned.1.call-start = ((), (), s32[]{:S(2)}) async-start(), calls=%async_computation.5 | async-start | bytes 131072 | tf_op jit(solution)/shard_map/psum | solution.py:59
  9.6 2.9 copy-start.3
  247.5 512.5 %all-gather.11.cloned.1.call-start = ((), (), s32[]{:S(2)}) async-start(), calls=%async_computation.4 | async-start | bytes 17825792 | tf_op jit(solution)/shard_map/all_gather | solution.py:98
  351.1 2.6 copy-start
  364.5 2.4 copy-start.1
  366.8 2.6 copy-start
  380.7 2.7 copy-start.1
  383.4 2.6 copy-start
  397.2 2.7 copy-start.1
  399.9 2.6 copy-start
  413.7 2.7 copy-start.1
  416.4 2.6 copy-start
  430.2 2.7 copy-start.1
  432.9 2.6 copy-start
  446.8 2.7 copy-start.1
  449.5 2.6 copy-start
  463.3 2.7 copy-start.1
  466.0 2.6 copy-start
  479.8 2.7 copy-start.1
  486.2 943.4 %all-gather.9.cloned.1.call-start = ((), (), s32[]{:S(2)}) async-start(), calls=%async_computation.3 | async-start | bytes 71303168 | tf_op jit(solution)/shard_map/all_gather | solution.py:89
Sparse Core Ops, SparseCore 0:
  10.8 61.5 all-gather.6
  75.1 59.1 all-gather.4
  247.6 103.3 all-reduce.2
  486.3 273.6 all-gather.10
  762.6 666.8 all-gather.8
